TPU v7x, 32 devices: a whole 2x2x4 slice. The times are simulated.
32 devices in a mesh: store: 8 (over z, y), seq: 4 (over x, core).
Axes of the slice: x: 2, y: 2, z: 4, core: 2. Of those that a mesh axis runs over, the one named last changes fastest.
Arguments:
- store_kv: bfloat16 [64, 320, 2048], P('store', 'seq'), may hold values from -8 to 8
- span_len: int32 [8, 16], replicated, may hold values from 37 to 80, as said below
- span_shard: int32 [8, 8], replicated, may hold values from 0 to 7, each once within a row
- q_sel: bfloat16 [8, 256, 8192], P('store', 'seq'), may hold values from -8 to 8
- fresh_kv: bfloat16 [8, 256, 2048], P('store', 'seq'), may hold values from -8 to 8
- sel_pos: int32 [8, 256], P('store', 'seq'), may hold values from -1 to 1023, as said below
Outputs:
- blended_kv: bfloat16 [8, 1024, 2048], P('store', 'seq')
- attn_out: bfloat16 [8, 256, 8192], P('store', 'seq')
Inputs may be any that keep to these rules, and one draw needn't show every extreme that they name: `span_len`: each row sums to 1024, and its largest entry is 80. `span_shard`: each row names every store shard once. `sel_pos`: on seq index q, the 64 slots of a request hold distinct positions from q * 256 to (q + 1) * 256 - 1 in rising order, then -1 in unused slots; at least 2 slots are used, and in every draw some device uses all 64.
All inputs are finite; a program needn't handle non-finite values.
Results may differ from a plain program's by a relative error of at most 0.007.
Values may be sent and summed in bfloat16 or wider, within the bound.
A program may use at most 192 MiB of HBM per device.

v0:
```python
import functools
import math

import jax
import jax.numpy as jnp
import numpy as np
from jax import lax
from jax.experimental import pallas as pl
from jax.experimental.pallas import tpu as pltpu
from jax.sharding import PartitionSpec as P

HEADS = 64
KV_HEADS = 8
D_HEAD = 128
GROUPS = HEADS // KV_HEADS
KV_WIDTH = KV_HEADS * D_HEAD
ROPE_BASE = 500000.0
CHUNKS = 8
LAG = 2
HPC = KV_HEADS // CHUNKS
CW = HPC * D_HEAD
F32 = jnp.float32
MESH = pl.DeviceIdType.MESH


def iota(shape, axis):
    return lax.broadcasted_iota(jnp.int32, shape, axis)


def own_row(ref, row):
    table = ref[...].astype(F32)
    return jnp.sum(jnp.where(iota(table.shape, 0) == row, table, 0.0), axis=0, keepdims=True)


def column(row):
    n = row.shape[1]
    square = (n, n)
    return jnp.sum(jnp.where(iota(square, 0) == iota(square, 1), row, 0.0), axis=1, keepdims=True)


def kernel(
    n_store, n_seq,
    store_ref, len_ref, shard_ref, inv_ref, q_ref, fresh_ref, sel_ref,
    kv_out, attn_out,
    landing, relay_in, merged, far, kv_all, qv, ov, pick, relay_pick, fresh_pick, is_fresh, cosine, sine, limit,
    fetch_send, fetch_recv, relay_send, relay_recv, merged_send, far_recv,
    own_sem, q_sem, gather_send, gather_recv,
    forward_send, pair_send, kv_sem, ov_sem,
):
    me = lax.axis_index("store")
    stripe = lax.axis_index("seq")
    slot_rows = store_ref.shape[1]
    tok = kv_out.shape[1]
    sel = sel_ref.shape[1]
    n_chips = n_seq // 2
    chip = stripe // 2
    core = stripe % 2
    sibling = chip * 2 + (1 - core)
    n_half = n_store // 2
    ny = n_store // 4
    half = me // n_half
    local = me % n_half
    lane = me % ny
    relay_row = 1 + half
    is_relay = me // ny == relay_row

    barrier = pltpu.get_barrier_semaphore()
    for d in range(1, n_store):
        pl.semaphore_signal(barrier, inc=1, device_id={"store": (me + d) % n_store}, device_id_type=MESH)
    for d in range(1, n_seq):
        pl.semaphore_signal(barrier, inc=1, device_id={"seq": (stripe + d) % n_seq}, device_id_type=MESH)
    pl.semaphore_wait(barrier, n_store + n_seq - 2)

    def part_cols(c, part):
        return pl.ds(pl.multiple_of(part * KV_WIDTH + c * CW, CW), CW)

    def fetch(c, src, dst, part):
        cols = part_cols(c, part)
        return pltpu.make_async_remote_copy(
            src_ref=store_ref.at[half * n_half + dst, :, cols],
            dst_ref=landing.at[src, :, cols],
            send_sem=fetch_send.at[c, dst, part],
            recv_sem=fetch_recv.at[c, src, part],
            device_id={"store": half * n_half + dst},
            device_id_type=MESH,
        )

    def far_request(y, j):
        return ((1 - half) * 2 + j) * ny + y

    def to_relay(c, src, y, j, part):
        cols = part_cols(c, part)
        return pltpu.make_async_remote_copy(
            src_ref=store_ref.at[far_request(y, j), :, cols],
            dst_ref=relay_in.at[j, src, :, cols],
            send_sem=relay_send.at[c, j, y, part],
            recv_sem=relay_recv.at[c, j, src, part],
            device_id={"store": relay_row * ny + y},
            device_id_type=MESH,
        )

    def relay_out(c, j):
        return pltpu.make_async_remote_copy(
            src_ref=merged.at[j, c],
            dst_ref=far.at[c],
            send_sem=merged_send.at[c, j],
            recv_sem=far_recv.at[c],
            device_id={"store": far_request(lane, j)},
            device_id_type=MESH,
        )

    own_copy = pltpu.make_async_copy(store_ref.at[me], landing.at[local], own_sem.at[0])
    q_copy = pltpu.make_async_copy(q_ref.at[0], qv, q_sem)

    def own_relay(j):
        return pltpu.make_async_copy(
            store_ref.at[far_request(lane, j)], relay_in.at[j, local], own_sem.at[1 + j]
        )

    def each_to_relay(c, act):
        for j in range(2):
            for part in range(2):
                @pl.when(jnp.logical_not(is_relay))
                def _():
                    act(to_relay(c, local, lane, j, part))

                for d in range(1, ny):
                    act(to_relay(c, local, (lane + d) % ny, j, part))

    def issue(c, carry):
        each_to_relay(c, lambda copy: copy.start())
        for d in range(1, n_half):
            for part in range(2):
                fetch(c, local, (local + d) % n_half, part).start()
        return carry

    lax.fori_loop(0, CHUNKS, issue, 0)
    own_copy.start()

    @pl.when(is_relay)
    def _():
        for j in range(2):
            own_relay(j).start()

    q_copy.start()

    first = (stripe * tok).astype(F32)
    n_span = len_ref.shape[1]

    def locate(request):
        lengths = own_row(len_ref, request)
        square = (n_span, n_span)
        starts = jnp.sum(
            jnp.where(iota(square, 0) < iota(square, 1), column(lengths), 0.0), axis=0, keepdims=True
        )
        shards = column(own_row(shard_ref, request))
        spread = (n_store, n_span)
        holders = jnp.sum(
            jnp.where(iota(spread, 1) % n_store == iota(spread, 0), shards, 0.0), axis=0, keepdims=True
        )
        grid = (tok, n_span)
        position = iota(grid, 0).astype(F32) + first
        which = jnp.sum(jnp.where(position >= starts, 1.0, 0.0), axis=1, keepdims=True) - 1.0
        picked = iota(grid, 1).astype(F32) == which
        holder = jnp.sum(jnp.where(picked, holders, 0.0), axis=1, keepdims=True)
        start = jnp.sum(jnp.where(picked, starts, 0.0), axis=1, keepdims=True)
        row = iota((tok, 1), 0).astype(F32) + first - jnp.maximum(start, first)
        target = (holder - (half * n_half).astype(F32)) * slot_rows + row
        chosen = jnp.where(iota(pick.shape, 1).astype(F32) == target, 1.0, 0.0)
        return chosen.astype(jnp.bfloat16), start

    @pl.when(is_relay)
    def _():
        for j in range(2):
            relay_pick[j] = locate(far_request(lane, j))[0]

    near, start = locate(me)
    pick[...] = near
    angle = start * inv_ref[...]
    cosine[...] = jnp.cos(angle)
    sine[...] = jnp.sin(angle) * jnp.where(iota((1, D_HEAD), 1) < D_HEAD // 2, -1.0, 1.0)
    chosen = sel_ref[...].astype(F32)
    matches = jnp.where(iota((tok, sel), 0).astype(F32) + first == chosen, 1.0, 0.0)
    fresh_pick[...] = matches.astype(jnp.bfloat16)
    is_fresh[...] = jnp.broadcast_to(jnp.sum(matches, axis=1, keepdims=True), is_fresh.shape)
    limit[...] = jnp.broadcast_to(column(chosen), limit.shape)

    def gather(c, peer_chip):
        block = kv_all.at[stripe, c]
        return pltpu.make_async_remote_copy(
            src_ref=block, dst_ref=block,
            send_sem=gather_send.at[c, peer_chip], recv_sem=gather_recv.at[c, stripe],
            device_id={"seq": peer_chip * 2 + core}, device_id_type=MESH,
        )

    def arrival(c, source):
        block = kv_all.at[source, c]
        return pltpu.make_async_remote_copy(
            src_ref=block, dst_ref=block,
            send_sem=forward_send.at[c, source // 2], recv_sem=gather_recv.at[c, source],
            device_id={"seq": sibling}, device_id_type=MESH,
        )

    def pair(c):
        block = kv_all.at[stripe, c]
        return pltpu.make_async_remote_copy(
            src_ref=block, dst_ref=block,
            send_sem=pair_send.at[c], recv_sem=gather_recv.at[c, stripe],
            device_id={"seq": sibling}, device_id_type=MESH,
        )

    def kv_store(c, part):
        return pltpu.make_async_copy(
            kv_all.at[stripe, c, :, pl.ds(part * CW, CW)],
            kv_out.at[0, :, part_cols(c, part)],
            kv_sem.at[c, part],
        )

    def out_cols(c):
        width = HPC * GROUPS * D_HEAD
        return pl.ds(pl.multiple_of(c * width, width), width)

    def ov_store(c):
        return pltpu.make_async_copy(ov.at[:, out_cols(c)], attn_out.at[0, :, out_cols(c)], ov_sem.at[c])

    def blend(c):
        for part in range(2):
            cols = part_cols(c, part)
            slots = landing[:, :, cols].reshape(n_half * slot_rows, CW)
            cached = jnp.dot(pick[...], slots, preferred_element_type=F32)
            cached = cached + far[c, :, part * CW:(part + 1) * CW].astype(F32)
            fresh = jnp.dot(fresh_pick[...], fresh_ref[0, :, cols], preferred_element_type=F32)
            for i in range(HPC):
                lanes = slice(i * D_HEAD, (i + 1) * D_HEAD)
                x = cached[:, lanes]
                if part == 0:
                    x = x * cosine[...] + pltpu.roll(x, D_HEAD // 2, 1) * sine[...]
                x = jnp.where(is_fresh[...] > 0.0, fresh[:, lanes], x)
                at = part * CW + i * D_HEAD
                kv_all[stripe, c, :, at:at + D_HEAD] = x.astype(jnp.bfloat16)

    scale = math.log2(math.e) / math.sqrt(D_HEAD)
    contract = (((1,), (1,)), ((), ()))

    def attend(c):
        for i in range(HPC):
            base = (c * HPC + i) * GROUPS * D_HEAD
            wide = qv[:, pl.ds(pl.multiple_of(base, GROUPS * D_HEAD), GROUPS * D_HEAD)]
            q = jnp.concatenate(
                [wide[:, g * D_HEAD:(g + 1) * D_HEAD] for g in range(GROUPS)], axis=0
            )
            k_lanes = slice(i * D_HEAD, (i + 1) * D_HEAD)
            v_lanes = slice(CW + i * D_HEAD, CW + (i + 1) * D_HEAD)

            def scores_of(s):
                keys = kv_all[s, c, :, k_lanes]
                return lax.dot_general(q, keys, contract, preferred_element_type=F32) * scale

            scores = scores_of(stripe)
            keep = iota((sel, tok), 1).astype(F32) + first <= limit[:, 0:1]
            keep = jnp.concatenate([jnp.where(keep, 0.0, -1e30)] * GROUPS, axis=0)
            scores = jnp.where(keep < 0.0, -1e30, scores)
            top = jnp.max(scores, axis=1, keepdims=True)
            weights = jnp.exp2(scores - top)
            total = jnp.sum(weights, axis=1, keepdims=True)
            acc = jnp.dot(
                weights.astype(jnp.bfloat16), kv_all[stripe, c, :, v_lanes],
                preferred_element_type=F32,
            )

            def earlier(s, state):
                top, total, acc = state
                scores = scores_of(s)
                raised = jnp.maximum(top, jnp.max(scores, axis=1, keepdims=True))
                fade = jnp.exp2(top - raised)
                weights = jnp.exp2(scores - raised)
                total = total * fade + jnp.sum(weights, axis=1, keepdims=True)
                acc = acc * fade + jnp.dot(
                    weights.astype(jnp.bfloat16), kv_all[s, c, :, v_lanes],
                    preferred_element_type=F32,
                )
                return raised, total, acc

            top, total, acc = lax.fori_loop(0, stripe, earlier, (top, total, acc))
            normed = acc * (1.0 / total)
            live = limit[...] >= 0.0
            for g in range(GROUPS):
                part = jnp.where(live, normed[g * sel:(g + 1) * sel], 0.0)
                ov[:, pl.ds(pl.multiple_of(base + g * D_HEAD, D_HEAD), D_HEAD)] = part.astype(jnp.bfloat16)

    def relay(c):
        for j in range(2):
            for part in range(2):
                for d in range(1, n_half):
                    to_relay(c, (local + d) % n_half, lane, j, part).wait_recv()

        @pl.when(c == 0)
        def _():
            for j in range(2):
                own_relay(j).wait()

        for j in range(2):
            for part in range(2):
                slots = relay_in[j, :, :, part_cols(c, part)].reshape(n_half * slot_rows, CW)
                rows = jnp.dot(relay_pick[j], slots, preferred_element_type=F32)
                merged[j, c, :, part * CW:(part + 1) * CW] = rows.astype(jnp.bfloat16)
            relay_out(c, j).start()

    def step(t, carry):
        @pl.when((t < CHUNKS) & is_relay)
        def _():
            relay(t)

        c = t - LAG

        @pl.when((c >= 0) & (c < CHUNKS))
        def _():
            for d in range(1, n_half):
                for part in range(2):
                    fetch(c, (local + d) % n_half, local, part).wait_recv()

            relay_out(c, 0).wait_recv()

            @pl.when(c == 0)
            def _():
                own_copy.wait()
                q_copy.wait()

            blend(c)
            for b in range(1, n_chips):
                @pl.when(chip < b)
                def _():
                    gather(c, b).start()

            @pl.when(core == 0)
            def _():
                pair(c).start()

            for part in range(2):
                kv_store(c, part).start()

        @pl.when(c > 0)
        def _():
            last = c - 1
            for a in range(n_chips - 1):
                @pl.when(a < chip)
                def _():
                    arrival(last, a * 2 + 1 - core).wait_recv()

            @pl.when(core == 1)
            def _():
                arrival(last, chip * 2).wait_recv()

            attend(last)
            ov_store(last).start()

        @pl.when((c >= 0) & (c < CHUNKS))
        def _():
            for a in range(n_chips - 1):
                @pl.when(a < chip)
                def _():
                    arrival(c, a * 2 + core).wait_recv()
                    arrival(c, a * 2 + core).start()

        return carry

    lax.fori_loop(0, CHUNKS + LAG + 1, step, 0)

    def drain(c, carry):
        each_to_relay(c, lambda copy: copy.wait_send())
        for d in range(1, n_half):
            for part in range(2):
                fetch(c, local, (local + d) % n_half, part).wait_send()

        @pl.when(is_relay)
        def _():
            for j in range(2):
                relay_out(c, j).wait_send()

        for b in range(1, n_chips):
            @pl.when(chip < b)
            def _():
                gather(c, b).wait_send()

        @pl.when(core == 0)
        def _():
            pair(c).wait_send()

        for a in range(n_chips - 1):
            @pl.when(a < chip)
            def _():
                arrival(c, a * 2 + core).wait_send()

        for part in range(2):
            kv_store(c, part).wait()
        ov_store(c).wait()
        return carry

    lax.fori_loop(0, CHUNKS, drain, 0)


def on_device(n_store, n_seq, store_kv, span_len, span_shard, q_sel, fresh_kv, sel_pos):
    slot_rows = store_kv.shape[1]
    tok = 256
    sel = sel_pos.shape[1]
    half = np.arange(D_HEAD // 2, dtype=np.float64) * 2.0 / D_HEAD
    inverse = np.power(ROPE_BASE, -np.concatenate([half, half]))[None].astype(np.float32)
    hbm = pl.BlockSpec(memory_space=pl.ANY)
    vmem = pl.BlockSpec(memory_space=pltpu.VMEM)
    dma = pltpu.SemaphoreType.DMA
    bf16 = jnp.bfloat16
    n_chips = n_seq // 2
    n_half = n_store // 2
    return pl.pallas_call(
        functools.partial(kernel, n_store, n_seq),
        out_shape=(
            jax.ShapeDtypeStruct((1, tok, 2 * KV_WIDTH), bf16),
            jax.ShapeDtypeStruct((1, sel, HEADS * D_HEAD), bf16),
        ),
        in_specs=[hbm, vmem, vmem, vmem, hbm, vmem, vmem],
        out_specs=(hbm, hbm),
        scratch_shapes=[
            pltpu.VMEM((n_half, slot_rows, 2 * KV_WIDTH), bf16),
            pltpu.VMEM((2, n_half, slot_rows, 2 * KV_WIDTH), bf16),
            pltpu.VMEM((2, CHUNKS, tok, 2 * CW), bf16),
            pltpu.VMEM((CHUNKS, tok, 2 * CW), bf16),
            pltpu.VMEM((n_seq, CHUNKS, tok, 2 * CW), bf16),
            pltpu.VMEM((sel, HEADS * D_HEAD), bf16),
            pltpu.VMEM((sel, HEADS * D_HEAD), bf16),
            pltpu.VMEM((tok, n_half * slot_rows), bf16),
            pltpu.VMEM((2, tok, n_half * slot_rows), bf16),
            pltpu.VMEM((tok, sel), bf16),
            pltpu.VMEM((tok, D_HEAD), F32),
            pltpu.VMEM((tok, D_HEAD), F32),
            pltpu.VMEM((tok, D_HEAD), F32),
            pltpu.VMEM((sel, D_HEAD), F32),
            dma((CHUNKS, n_half, 2)),
            dma((CHUNKS, n_half, 2)),
            dma((CHUNKS, 2, n_store // 4, 2)),
            dma((CHUNKS, 2, n_half, 2)),
            dma((CHUNKS, 2)),
            dma((CHUNKS,)),
            dma((3,)),
            dma(()),
            dma((CHUNKS, n_chips)),
            dma((CHUNKS, n_seq)),
            dma((CHUNKS, n_chips)),
            dma((CHUNKS,)),
            dma((CHUNKS, 2)),
            dma((CHUNKS,)),
        ],
        compiler_params=pltpu.CompilerParams(
            collective_id=0, has_side_effects=True, vmem_limit_bytes=60 * 1024 * 1024
        ),
    )(store_kv, span_len, span_shard, jnp.asarray(inverse), q_sel, fresh_kv, sel_pos)


def solution(mesh):
    n_store, n_seq = mesh.shape["store"], mesh.shape["seq"]
    return jax.shard_map(
        functools.partial(on_device, n_store, n_seq),
        mesh=mesh,
        in_specs=(
            P("store", "seq", None),
            P(),
            P(),
            P("store", "seq", None),
            P("store", "seq", None),
            P("store", "seq"),
        ),
        out_specs=(P("store", "seq", None), P("store", "seq", None)),
        check_vma=False,
    )
```

profile of v0, /device:TPU:11, one launch (start us, length us, event | category | flops | bytes accessed | tf_op | source)
XLA Modules:
  0.0 73.2 jit_solution(3239602068959528543)
XLA Ops:
  0.6 69.2 %shard_map.86 = (bf16[1,256,2048]{2,1,0:T(8,128)(2,1)}, bf16[1,64,8192]{2,1,0:T(8,128)(2,1)}) custom-call(bf16[8,80,2048]{2,1,0:T(8,128)(2,1)} %store_ref.1, s32[8,16]{1,0:T(8,128)} %len_ref.1, s32[8,8]{1,0:T(8,128)} %shard_ref.1, f32[1,128]{1,0:T(1,128)} %constant.2.clone.inv_ref, bf16[1,64,8192]{2,1,0:T(8,128)(2,1)} %q_ref.1, ...), custom_call_target="tpu_custom_call" | custom-call | tf_op jit(solution)/shard_map/pallas_call | solution.py:414
  69.8 0.0 copy-start
  69.8 2.4 %copy.11 = bf16[1,256,2048]{2,1,0:T(8,128)(2,1)} copy(bf16[1,256,2048]{2,1,0:T(8,128)(2,1)} %get-tuple-element.4) | data formatting | bytes 2097152
  72.2 0.0 copy-done
  72.2 1.0 %copy.12 = bf16[1,64,8192]{2,1,0:T(8,128)(2,1)} copy(bf16[1,64,8192]{2,1,0:T(8,128)(2,1)S(1)} %copy-done) | data formatting | bytes 2097152
Async XLA Ops:
  69.8 2.4 %copy-start = (bf16[1,64,8192]{2,1,0:T(8,128)(2,1)S(1)}, bf16[1,64,8192]{2,1,0:T(8,128)(2,1)}, u32[]{:S(2)}) copy-start(bf16[1,64,8192]{2,1,0:T(8,128)(2,1)} %get-tuple-element.5) | copy-start | bytes 3145732
where the time goes:
time: 73.3 us; the launch traced here: 73.2 us
  Pallas kernels  69.2 us (94%)
  local copies, waits for them, and re-layouts  3.37 us (5%)
    pallas_call x1, Pallas kernels, on_device(): pl.pallas_call(functools.partial(kernel, n_store, n_seq), out_shape=(jax....  69.2 us
    unnamed x4, local copies, waits for them, and re-layouts  3.37 us

commit v1 on v0

--- a/solution.py
+++ b/solution.py
@@ -17,6 +17,8 @@
 ROPE_BASE = 500000.0
 CHUNKS = 8
 LAG = 2
+LEAD = 2
+SHORTEST, LONGEST = 37, 80
 HPC = KV_HEADS // CHUNKS
 CW = HPC * D_HEAD
 F32 = jnp.float32
@@ -38,12 +40,24 @@
     return jnp.sum(jnp.where(iota(square, 0) == iota(square, 1), row, 0.0), axis=1, keepdims=True)
 
 
+def frame_rows(n_store, slot_rows, tok):
+    half = n_store // 2
+    shortest = slot_rows * SHORTEST // LONGEST
+    window = 2 * tok
+    most, m = 0, 0
+    while window > m * half * shortest:
+        most = max(most, min((m + 1) * half * slot_rows, window - m * half * shortest))
+        m += 1
+    return min(tok, -(-most // 32) * 16)
+
+
 def kernel(
     n_store, n_seq,
     store_ref, len_ref, shard_ref, inv_ref, q_ref, fresh_ref, sel_ref,
     kv_out, attn_out,
-    landing, relay_in, merged, far, kv_all, qv, ov, pick, relay_pick, fresh_pick, is_fresh, cosine, sine, limit,
+    landing, relay_in, merged, far, kv_all, qv, ov, pick, far_pick, relay_pick, fresh_pick, tail_out, tail_in, is_fresh, cosine, sine, limit,
     fetch_send, fetch_recv, relay_send, relay_recv, merged_send, far_recv,
+    tail_send, tail_recv, spill_send, spill_recv,
     own_sem, q_sem, gather_send, gather_recv,
     forward_send, pair_send, kv_sem, ov_sem,
 ):
@@ -52,6 +66,8 @@
     slot_rows = store_ref.shape[1]
     tok = kv_out.shape[1]
     sel = sel_ref.shape[1]
+    keep_rows = merged.shape[2]
+    spill = tok - keep_rows
     n_chips = n_seq // 2
     chip = stripe // 2
     core = stripe % 2
@@ -102,10 +118,30 @@
     def relay_out(c, j):
         return pltpu.make_async_remote_copy(
             src_ref=merged.at[j, c],
-            dst_ref=far.at[c],
+            dst_ref=far.at[c, pl.ds(0, keep_rows)],
             send_sem=merged_send.at[c, j],
             recv_sem=far_recv.at[c],
             device_id={"store": far_request(lane, j)},
+            device_id_type=MESH,
+        )
+
+    def relay_tail(c, j):
+        return pltpu.make_async_remote_copy(
+            src_ref=tail_out.at[j, c],
+            dst_ref=tail_in.at[j, c],
+            send_sem=tail_send.at[c, j],
+            recv_sem=tail_recv.at[c, j],
+            device_id={"seq": sibling},
+            device_id_type=MESH,
+        )
+
+    def far_tail(c):
+        return pltpu.make_async_remote_copy(
+            src_ref=far.at[c, pl.ds(keep_rows - spill, spill)],
+            dst_ref=far.at[c, pl.ds(keep_rows, spill)],
+            send_sem=spill_send.at[c],
+            recv_sem=spill_recv.at[c],
+            device_id={"seq": sibling},
             device_id_type=MESH,
         )
 
@@ -127,14 +163,20 @@
                 for d in range(1, ny):
                     act(to_relay(c, local, (lane + d) % ny, j, part))
 
-    def issue(c, carry):
-        each_to_relay(c, lambda copy: copy.start())
-        for d in range(1, n_half):
-            for part in range(2):
-                fetch(c, local, (local + d) % n_half, part).start()
+    def issue(t, carry):
+        @pl.when(t < CHUNKS)
+        def _():
+            each_to_relay(t, lambda copy: copy.start())
+
+        @pl.when(t >= LEAD)
+        def _():
+            for d in range(1, n_half):
+                for part in range(2):
+                    fetch(t - LEAD, local, (local + d) % n_half, part).start()
+
         return carry
 
-    lax.fori_loop(0, CHUNKS, issue, 0)
+    lax.fori_loop(0, CHUNKS + LEAD, issue, 0)
     own_copy.start()
 
     @pl.when(is_relay)
@@ -167,15 +209,29 @@
         row = iota((tok, 1), 0).astype(F32) + first - jnp.maximum(start, first)
         target = (holder - (half * n_half).astype(F32)) * slot_rows + row
         chosen = jnp.where(iota(pick.shape, 1).astype(F32) == target, 1.0, 0.0)
-        return chosen.astype(jnp.bfloat16), start
+        side = jnp.where(holder >= n_half, 1.0, 0.0)
+        return chosen.astype(jnp.bfloat16), start, jnp.where(side == half.astype(F32), 1.0, 0.0)
+
+    def framed(member):
+        square = (tok, tok)
+        before = jnp.where(iota(square, 1) < iota(square, 0), 1.0, 0.0).astype(jnp.bfloat16)
+        wide = jnp.broadcast_to(member, (tok, D_HEAD)).astype(jnp.bfloat16)
+        rank = jnp.dot(before, wide, preferred_element_type=F32)[:, 0:1]
+        at = jnp.where(rank < keep_rows, rank, float(2 * keep_rows + spill - 1) - rank)
+        at = jnp.where(member > 0.0, at, -1.0)
+        return jnp.where(iota(square, 1).astype(F32) == at, 1.0, 0.0).astype(jnp.bfloat16)
 
     @pl.when(is_relay)
     def _():
         for j in range(2):
-            relay_pick[j] = locate(far_request(lane, j))[0]
-
-    near, start = locate(me)
+            chosen, _, member = locate(far_request(lane, j))
+            relay_pick[j] = lax.dot_general(
+                framed(member), chosen, (((0,), (0,)), ((), ())), preferred_element_type=F32
+            ).astype(jnp.bfloat16)
+
+    near, start, member = locate(me)
     pick[...] = near
+    far_pick[...] = framed(1.0 - member)
     angle = start * inv_ref[...]
     cosine[...] = jnp.cos(angle)
     sine[...] = jnp.sin(angle) * jnp.where(iota((1, D_HEAD), 1) < D_HEAD // 2, -1.0, 1.0)
@@ -228,7 +284,9 @@
             cols = part_cols(c, part)
             slots = landing[:, :, cols].reshape(n_half * slot_rows, CW)
             cached = jnp.dot(pick[...], slots, preferred_element_type=F32)
-            cached = cached + far[c, :, part * CW:(part + 1) * CW].astype(F32)
+            cached = cached + jnp.dot(
+                far_pick[...], far[c, :, part * CW:(part + 1) * CW], preferred_element_type=F32
+            )
             fresh = jnp.dot(fresh_pick[...], fresh_ref[0, :, cols], preferred_element_type=F32)
             for i in range(HPC):
                 lanes = slice(i * D_HEAD, (i + 1) * D_HEAD)
@@ -303,7 +361,17 @@
             for part in range(2):
                 slots = relay_in[j, :, :, part_cols(c, part)].reshape(n_half * slot_rows, CW)
                 rows = jnp.dot(relay_pick[j], slots, preferred_element_type=F32)
-                merged[j, c, :, part * CW:(part + 1) * CW] = rows.astype(jnp.bfloat16)
+                cols = slice(part * CW, (part + 1) * CW)
+                merged[j, c, :, cols] = rows[:keep_rows].astype(jnp.bfloat16)
+                if spill:
+                    tail_out[j, c, :, cols] = rows[keep_rows:].astype(jnp.bfloat16)
+            if spill:
+                relay_tail(c, j).start()
+
+        for j in range(2):
+            if spill:
+                relay_tail(c, j).wait_recv()
+                merged[j, c, keep_rows - spill:] = merged[j, c, keep_rows - spill:] + tail_in[j, c]
             relay_out(c, j).start()
 
     def step(t, carry):
@@ -312,20 +380,41 @@
             relay(t)
 
         c = t - LAG
+
+        @pl.when((c >= 0) & (c < CHUNKS))
+        def _():
+            relay_out(c, 0).wait_recv()
+            if spill:
+                far_tail(c).start()
+
+        @pl.when(c > 0)
+        def _():
+            last = c - 1
+            for a in range(n_chips - 1):
+                @pl.when(a < chip)
+                def _():
+                    arrival(last, a * 2 + 1 - core).wait_recv()
+
+            @pl.when(core == 1)
+            def _():
+                arrival(last, chip * 2).wait_recv()
+
+            attend(last)
+            ov_store(last).start()
 
         @pl.when((c >= 0) & (c < CHUNKS))
         def _():
             for d in range(1, n_half):
                 for part in range(2):
                     fetch(c, (local + d) % n_half, local, part).wait_recv()
-
-            relay_out(c, 0).wait_recv()
 
             @pl.when(c == 0)
             def _():
                 own_copy.wait()
                 q_copy.wait()
 
+            if spill:
+                far_tail(c).wait_recv()
             blend(c)
             for b in range(1, n_chips):
                 @pl.when(chip < b)
@@ -339,23 +428,6 @@
             for part in range(2):
                 kv_store(c, part).start()
 
-        @pl.when(c > 0)
-        def _():
-            last = c - 1
-            for a in range(n_chips - 1):
-                @pl.when(a < chip)
-                def _():
-                    arrival(last, a * 2 + 1 - core).wait_recv()
-
-            @pl.when(core == 1)
-            def _():
-                arrival(last, chip * 2).wait_recv()
-
-            attend(last)
-            ov_store(last).start()
-
-        @pl.when((c >= 0) & (c < CHUNKS))
-        def _():
             for a in range(n_chips - 1):
                 @pl.when(a < chip)
                 def _():
@@ -375,7 +447,12 @@
         @pl.when(is_relay)
         def _():
             for j in range(2):
+                if spill:
+                    relay_tail(c, j).wait_send()
                 relay_out(c, j).wait_send()
+
+        if spill:
+            far_tail(c).wait_send()
 
         for b in range(1, n_chips):
             @pl.when(chip < b)
@@ -411,6 +488,8 @@
     bf16 = jnp.bfloat16
     n_chips = n_seq // 2
     n_half = n_store // 2
+    keep_rows = frame_rows(n_store, slot_rows, tok)
+    spill = tok - keep_rows
     return pl.pallas_call(
         functools.partial(kernel, n_store, n_seq),
         out_shape=(
@@ -422,14 +501,17 @@
         scratch_shapes=[
             pltpu.VMEM((n_half, slot_rows, 2 * KV_WIDTH), bf16),
             pltpu.VMEM((2, n_half, slot_rows, 2 * KV_WIDTH), bf16),
-            pltpu.VMEM((2, CHUNKS, tok, 2 * CW), bf16),
+            pltpu.VMEM((2, CHUNKS, keep_rows, 2 * CW), bf16),
             pltpu.VMEM((CHUNKS, tok, 2 * CW), bf16),
             pltpu.VMEM((n_seq, CHUNKS, tok, 2 * CW), bf16),
             pltpu.VMEM((sel, HEADS * D_HEAD), bf16),
             pltpu.VMEM((sel, HEADS * D_HEAD), bf16),
             pltpu.VMEM((tok, n_half * slot_rows), bf16),
+            pltpu.VMEM((tok, tok), bf16),
             pltpu.VMEM((2, tok, n_half * slot_rows), bf16),
             pltpu.VMEM((tok, sel), bf16),
+            pltpu.VMEM((2, CHUNKS, spill, 2 * CW), bf16),
+            pltpu.VMEM((2, CHUNKS, spill, 2 * CW), bf16),
             pltpu.VMEM((tok, D_HEAD), F32),
             pltpu.VMEM((tok, D_HEAD), F32),
             pltpu.VMEM((tok, D_HEAD), F32),
@@ -439,6 +521,10 @@
             dma((CHUNKS, 2, n_store // 4, 2)),
             dma((CHUNKS, 2, n_half, 2)),
             dma((CHUNKS, 2)),
+            dma((CHUNKS,)),
+            dma((CHUNKS, 2)),
+            dma((CHUNKS, 2)),
+            dma((CHUNKS,)),
             dma((CHUNKS,)),
             dma((3,)),
             dma(()),

time: 73.3 us -> 72.5 us (0.989)
  Pallas kernels: 69.2 us -> 68.3 us
    pallas_call x1, Pallas kernels: 69.2 us -> 68.3 us  [on_device(): pl.pallas_call(functools.partial(kernel, n_store, n_seq), out_shape=(jax....]
where the time goes in v1:
time: 72.5 us; the launch traced here: 72.4 us
  Pallas kernels  68.3 us (94%)
  local copies, waits for them, and re-layouts  3.37 us (5%)
    pallas_call x1, Pallas kernels, on_device(): pl.pallas_call(functools.partial(kernel, n_store, n_seq), out_shape=(jax....  68.3 us
    unnamed x4, local copies, waits for them, and re-layouts  3.37 us

profile of v1, /device:TPU:11, one launch (start us, length us, event | category | flops | bytes accessed | tf_op | source)
XLA Modules:
  0.0 72.4 jit_solution(2553081968114748091)
XLA Ops:
  0.6 68.3 %shard_map.86 = (bf16[1,256,2048]{2,1,0:T(8,128)(2,1)}, bf16[1,64,8192]{2,1,0:T(8,128)(2,1)}) custom-call(bf16[8,80,2048]{2,1,0:T(8,128)(2,1)} %store_ref.1, s32[8,16]{1,0:T(8,128)} %len_ref.1, s32[8,8]{1,0:T(8,128)} %shard_ref.1, f32[1,128]{1,0:T(1,128)} %constant.2.clone.inv_ref, bf16[1,64,8192]{2,1,0:T(8,128)(2,1)} %q_ref.1, ...), custom_call_target="tpu_custom_call" | custom-call | tf_op jit(solution)/shard_map/pallas_call | solution.py:493
  69.0 0.0 copy-start
  69.0 2.4 %copy.11 = bf16[1,256,2048]{2,1,0:T(8,128)(2,1)} copy(bf16[1,256,2048]{2,1,0:T(8,128)(2,1)} %get-tuple-element.4) | data formatting | bytes 2097152
  71.4 0.0 copy-done
  71.4 1.0 %copy.12 = bf16[1,64,8192]{2,1,0:T(8,128)(2,1)} copy(bf16[1,64,8192]{2,1,0:T(8,128)(2,1)S(1)} %copy-done) | data formatting | bytes 2097152
Async XLA Ops:
  69.0 2.4 %copy-start = (bf16[1,64,8192]{2,1,0:T(8,128)(2,1)S(1)}, bf16[1,64,8192]{2,1,0:T(8,128)(2,1)}, u32[]{:S(2)}) copy-start(bf16[1,64,8192]{2,1,0:T(8,128)(2,1)} %get-tuple-element.5) | copy-start | bytes 3145732

commit v2 on v1

v2 whole, which is shorter than its diff:
```python
import functools
import math

import jax
import jax.numpy as jnp
import numpy as np
from jax import lax
from jax.experimental import pallas as pl
from jax.experimental.pallas import tpu as pltpu
from jax.sharding import PartitionSpec as P

HEADS = 64
KV_HEADS = 8
D_HEAD = 128
GROUPS = HEADS // KV_HEADS
KV_WIDTH = KV_HEADS * D_HEAD
ROPE_BASE = 500000.0
CHUNKS = KV_HEADS
LAG = 2
LEAD = 2
SHORTEST, LONGEST = 37, 80
CW = D_HEAD
F32 = jnp.float32
MESH = pl.DeviceIdType.MESH


def iota(shape, axis):
    return lax.broadcasted_iota(jnp.int32, shape, axis)


def own_row(ref, row):
    table = ref[...].astype(F32)
    return jnp.sum(jnp.where(iota(table.shape, 0) == row, table, 0.0), axis=0, keepdims=True)


def column(row):
    n = row.shape[1]
    square = (n, n)
    return jnp.sum(jnp.where(iota(square, 0) == iota(square, 1), row, 0.0), axis=1, keepdims=True)


def frame_rows(n_store, slot_rows, tok):
    half = n_store // 2
    shortest = slot_rows * SHORTEST // LONGEST
    window = 2 * tok
    most, m = 0, 0
    while window > m * half * shortest:
        most = max(most, min((m + 1) * half * slot_rows, window - m * half * shortest))
        m += 1
    return min(tok, -(-most // 32) * 16)


def kernel(
    n_store, n_seq,
    store_ref, len_hbm, shard_hbm, inv_hbm, q_ref, fresh_hbm, sel_hbm,
    kv_out, attn_out,
    len_ref, shard_ref, inv_ref, fresh_ref, sel_ref,
    landing, relay_in, merged, far, kv_all, qv, scores, pick, far_pick, relay_pick, fresh_pick, tail_out, tail_in, is_fresh, cosine, sine, limit,
    fetch_send, fetch_recv, relay_send, relay_recv, merged_send, far_recv,
    tail_send, tail_recv, spill_send, spill_recv,
    own_sem, q_sem, gather_send, direct_recv, sibling_recv, pair_recv,
    forward_send, pair_send, load_sem,
):
    me = lax.axis_index("store")
    stripe = lax.axis_index("seq")
    slot_rows = store_ref.shape[1]
    tok = kv_out.shape[1]
    sel = sel_ref.shape[1]
    keep_rows = merged.shape[2]
    spill = tok - keep_rows
    n_chips = n_seq // 2
    chip = stripe // 2
    core = stripe % 2
    sibling = chip * 2 + (1 - core)
    n_half = n_store // 2
    ny = n_store // 4
    half = me // n_half
    local = me % n_half
    lane = me % ny
    relay_row = 1 + half
    is_relay = me // ny == relay_row

    barrier = pltpu.get_barrier_semaphore()
    for d in range(1, n_half):
        peer = half * n_half + (local + d) % n_half
        pl.semaphore_signal(barrier, inc=1, device_id={"store": peer}, device_id_type=MESH)
    pl.semaphore_signal(barrier, inc=1, device_id={"store": (2 - half) * ny + lane}, device_id_type=MESH)
    for d in range(1, n_seq):
        pl.semaphore_signal(barrier, inc=1, device_id={"seq": (stripe + d) % n_seq}, device_id_type=MESH)

    loads = [
        pltpu.make_async_copy(src, dst, load_sem.at[i])
        for i, (src, dst) in enumerate([
            (len_hbm, len_ref), (shard_hbm, shard_ref), (inv_hbm, inv_ref), (sel_hbm, sel_ref), (fresh_hbm, fresh_ref),
        ])
    ]
    for load in loads:
        load.start()

    peers = n_half + n_seq - 2

    @pl.when(is_relay)
    def _():
        pl.semaphore_wait(barrier, peers + 2)

    @pl.when(jnp.logical_not(is_relay))
    def _():
        pl.semaphore_wait(barrier, peers)

    def part_cols(c, part):
        return pl.ds(pl.multiple_of(part * KV_WIDTH + c * CW, CW), CW)

    def fetch(c, src, dst, part):
        cols = part_cols(c, part)
        return pltpu.make_async_remote_copy(
            src_ref=store_ref.at[half * n_half + dst, :, cols],
            dst_ref=landing.at[src, :, cols],
            send_sem=fetch_send,
            recv_sem=fetch_recv.at[c, part],
            device_id={"store": half * n_half + dst},
            device_id_type=MESH,
        )

    def far_request(y, j):
        return ((1 - half) * 2 + j) * ny + y

    def to_relay(c, src, y, j, part):
        cols = part_cols(c, part)
        return pltpu.make_async_remote_copy(
            src_ref=store_ref.at[far_request(y, j), :, cols],
            dst_ref=relay_in.at[j, src, :, cols],
            send_sem=relay_send,
            recv_sem=relay_recv.at[c, part],
            device_id={"store": relay_row * ny + y},
            device_id_type=MESH,
        )

    def relay_out(c, j):
        return pltpu.make_async_remote_copy(
            src_ref=merged.at[j, c],
            dst_ref=far.at[c, pl.ds(0, keep_rows)],
            send_sem=merged_send,
            recv_sem=far_recv.at[c],
            device_id={"store": far_request(lane, j)},
            device_id_type=MESH,
        )

    def relay_tail(c, j):
        return pltpu.make_async_remote_copy(
            src_ref=tail_out.at[j, c],
            dst_ref=tail_in.at[j, c],
            send_sem=tail_send,
            recv_sem=tail_recv.at[c],
            device_id={"seq": sibling},
            device_id_type=MESH,
        )

    def far_tail(c):
        return pltpu.make_async_remote_copy(
            src_ref=far.at[c, pl.ds(keep_rows - spill, spill)],
            dst_ref=far.at[c, pl.ds(keep_rows, spill)],
            send_sem=spill_send,
            recv_sem=spill_recv.at[c],
            device_id={"seq": sibling},
            device_id_type=MESH,
        )

    own_copy = pltpu.make_async_copy(store_ref.at[me], landing.at[local], own_sem.at[0])
    q_copy = pltpu.make_async_copy(q_ref.at[0], qv, q_sem)

    def own_relay(j):
        return pltpu.make_async_copy(
            store_ref.at[far_request(lane, j)], relay_in.at[j, local], own_sem.at[1 + j]
        )

    def each_to_relay(c, act):
        for j in range(2):
            for part in range(2):
                @pl.when(jnp.logical_not(is_relay))
                def _():
                    act(to_relay(c, local, lane, j, part))

                for d in range(1, ny):
                    act(to_relay(c, local, (lane + d) % ny, j, part))

    def issue(t, carry):
        @pl.when(t < CHUNKS)
        def _():
            each_to_relay(t, lambda copy: copy.start())

        @pl.when(t >= LEAD)
        def _():
            for d in range(1, n_half):
                for part in range(2):
                    fetch(t - LEAD, local, (local + d) % n_half, part).start()

        return carry

    lax.fori_loop(0, CHUNKS + LEAD, issue, 0)
    own_copy.start()

    @pl.when(is_relay)
    def _():
        for j in range(2):
            own_relay(j).start()

    q_copy.start()

    for load in loads:
        load.wait()

    first = (stripe * tok).astype(F32)
    n_span = len_ref.shape[1]

    def locate(request):
        lengths = own_row(len_ref, request)
        square = (n_span, n_span)
        starts = jnp.sum(
            jnp.where(iota(square, 0) < iota(square, 1), column(lengths), 0.0), axis=0, keepdims=True
        )
        shards = column(own_row(shard_ref, request))
        spread = (n_store, n_span)
        holders = jnp.sum(
            jnp.where(iota(spread, 1) % n_store == iota(spread, 0), shards, 0.0), axis=0, keepdims=True
        )
        grid = (tok, n_span)
        position = iota(grid, 0).astype(F32) + first
        which = jnp.sum(jnp.where(position >= starts, 1.0, 0.0), axis=1, keepdims=True) - 1.0
        picked = iota(grid, 1).astype(F32) == which
        holder = jnp.sum(jnp.where(picked, holders, 0.0), axis=1, keepdims=True)
        start = jnp.sum(jnp.where(picked, starts, 0.0), axis=1, keepdims=True)
        row = iota((tok, 1), 0).astype(F32) + first - jnp.maximum(start, first)
        target = (holder - (half * n_half).astype(F32)) * slot_rows + row
        chosen = jnp.where(iota(pick.shape, 1).astype(F32) == target, 1.0, 0.0)
        side = jnp.where(holder >= n_half, 1.0, 0.0)
        return chosen.astype(jnp.bfloat16), start, jnp.where(side == half.astype(F32), 1.0, 0.0)

    def framed(member):
        square = (tok, tok)
        before = jnp.where(iota(square, 1) < iota(square, 0), 1.0, 0.0).astype(jnp.bfloat16)
        wide = jnp.broadcast_to(member, (tok, D_HEAD)).astype(jnp.bfloat16)
        rank = jnp.dot(before, wide, preferred_element_type=F32)[:, 0:1]
        at = jnp.where(rank < keep_rows, rank, float(2 * keep_rows + spill - 1) - rank)
        at = jnp.where(member > 0.0, at, -1.0)
        return jnp.where(iota(square, 1).astype(F32) == at, 1.0, 0.0).astype(jnp.bfloat16)

    @pl.when(is_relay)
    def _():
        for j in range(2):
            chosen, _, member = locate(far_request(lane, j))
            relay_pick[j] = lax.dot_general(
                framed(member), chosen, (((0,), (0,)), ((), ())), preferred_element_type=F32
            ).astype(jnp.bfloat16)

    near, start, member = locate(me)
    pick[...] = near
    far_pick[...] = framed(1.0 - member)
    angle = start * inv_ref[...]
    cosine[...] = jnp.cos(angle)
    sine[...] = jnp.sin(angle) * jnp.where(iota((1, D_HEAD), 1) < D_HEAD // 2, -1.0, 1.0)
    chosen = sel_ref[...].astype(F32)
    matches = jnp.where(iota((tok, sel), 0).astype(F32) + first == chosen, 1.0, 0.0)
    fresh_pick[...] = matches.astype(jnp.bfloat16)
    is_fresh[...] = jnp.broadcast_to(jnp.sum(matches, axis=1, keepdims=True), is_fresh.shape)
    limit[...] = jnp.broadcast_to(column(chosen), limit.shape)

    def gather(c, peer_chip, part):
        block = kv_all.at[stripe, c, part]
        return pltpu.make_async_remote_copy(
            src_ref=block, dst_ref=block,
            send_sem=gather_send.at[peer_chip], recv_sem=direct_recv.at[c, chip, part],
            device_id={"seq": peer_chip * 2 + core}, device_id_type=MESH,
        )

    def direct(c, a, part):
        block = kv_all.at[a * 2 + core, c, part]
        return pltpu.make_async_copy(block, block, direct_recv.at[c, a, part])

    def passed_on(c, a, part):
        block = kv_all.at[a * 2 + core, c, part]
        return pltpu.make_async_remote_copy(
            src_ref=block, dst_ref=block,
            send_sem=forward_send.at[a], recv_sem=sibling_recv.at[c, a, part],
            device_id={"seq": sibling}, device_id_type=MESH,
        )

    def pair(c, part):
        block = kv_all.at[stripe, c, part]
        return pltpu.make_async_remote_copy(
            src_ref=block, dst_ref=block,
            send_sem=pair_send, recv_sem=pair_recv.at[c, part],
            device_id={"seq": sibling}, device_id_type=MESH,
        )

    def settle(ref, sem):
        pltpu.make_async_copy(ref, ref, sem).wait()

    def blend(c, part):
        cols = part_cols(c, part)
        slots = landing[:, :, cols].reshape(n_half * slot_rows, CW)
        x = jnp.dot(pick[...], slots, preferred_element_type=F32)
        x = x + jnp.dot(far_pick[...], far[c, :, part * CW:(part + 1) * CW], preferred_element_type=F32)
        fresh = jnp.dot(fresh_pick[...], fresh_ref[0, :, cols], preferred_element_type=F32)
        if part == 0:
            x = x * cosine[...] + pltpu.roll(x, D_HEAD // 2, 1) * sine[...]
        x = jnp.where(is_fresh[...] > 0.0, fresh, x)
        x = x.astype(jnp.bfloat16)
        kv_all[stripe, c, part] = x
        kv_out[0, :, cols] = x

    scale = math.log2(math.e) / math.sqrt(D_HEAD)
    contract = (((1,), (1,)), ((), ()))

    def forward(c, part):
        for a in range(n_chips - 1):
            @pl.when(a < chip)
            def _():
                direct(c, a, part).wait()
                passed_on(c, a, part).start()

    def await_sibling(c, part):
        for a in range(n_chips - 1):
            @pl.when(a < chip)
            def _():
                settle(kv_all.at[a * 2 + 1 - core, c, part], sibling_recv.at[c, a, part])

        @pl.when(core == 1)
        def _():
            settle(kv_all.at[chip * 2, c, part], pair_recv.at[c, part])

    def peak_of(x):
        top = x[:, :D_HEAD]
        for i in range(1, tok // D_HEAD):
            top = jnp.maximum(top, x[:, i * D_HEAD:(i + 1) * D_HEAD])
        return top

    def attend(c):
        base = c * GROUPS * D_HEAD
        wide = qv[:, pl.ds(pl.multiple_of(base, GROUPS * D_HEAD), GROUPS * D_HEAD)]
        q = jnp.concatenate([wide[:, g * D_HEAD:(g + 1) * D_HEAD] for g in range(GROUPS)], axis=0)

        def scores_of(s):
            return lax.dot_general(q, kv_all[s, c, 0], contract, preferred_element_type=F32)

        own = scores_of(stripe)
        keep = iota((sel, tok), 1).astype(F32) + first <= limit[:, 0:1]
        keep = jnp.concatenate([jnp.where(keep, 0.0, -1e30)] * GROUPS, axis=0)
        own = jnp.where(keep < 0.0, -1e30, own)
        scores[stripe] = own
        await_sibling(c, 0)

        def score(s, top):
            x = scores_of(s)
            scores[s] = x
            return jnp.maximum(top, peak_of(x))

        top = lax.fori_loop(0, stripe, score, peak_of(own))
        top = jnp.max(top, axis=1, keepdims=True) * scale
        forward(c, 1)
        ones = jnp.ones((tok, D_HEAD), jnp.bfloat16)

        def weighted(s):
            weights = jnp.exp2(scores[s] * scale - top).astype(jnp.bfloat16)
            return jnp.dot(
                weights, jnp.concatenate([kv_all[s, c, 1], ones], axis=1), preferred_element_type=F32
            )

        acc = weighted(stripe)
        await_sibling(c, 1)
        acc = lax.fori_loop(0, stripe, lambda s, acc: acc + weighted(s), acc)
        normed = acc[:, :D_HEAD] * (1.0 / acc[:, D_HEAD:])
        live = limit[...] >= 0.0
        for g in range(GROUPS):
            part = jnp.where(live, normed[g * sel:(g + 1) * sel], 0.0)
            attn_out[0, :, pl.ds(pl.multiple_of(base + g * D_HEAD, D_HEAD), D_HEAD)] = part.astype(jnp.bfloat16)

    def relay(c):
        for part in range(2):
            settle(relay_in.at[:, pl.ds(0, n_half - 1), :, part_cols(c, part)], relay_recv.at[c, part])

        @pl.when(c == 0)
        def _():
            for j in range(2):
                own_relay(j).wait()

        for j in range(2):
            for part in range(2):
                slots = relay_in[j, :, :, part_cols(c, part)].reshape(n_half * slot_rows, CW)
                rows = jnp.dot(relay_pick[j], slots, preferred_element_type=F32)
                cols = slice(part * CW, (part + 1) * CW)
                merged[j, c, :, cols] = rows[:keep_rows].astype(jnp.bfloat16)
                if spill:
                    tail_out[j, c, :, cols] = rows[keep_rows:].astype(jnp.bfloat16)
            if spill:
                relay_tail(c, j).start()

        if spill:
            settle(tail_in.at[:, c], tail_recv.at[c])
        for j in range(2):
            if spill:
                merged[j, c, keep_rows - spill:] = merged[j, c, keep_rows - spill:] + tail_in[j, c]
            relay_out(c, j).start()

    def step(t, carry):
        @pl.when((t < CHUNKS) & is_relay)
        def _():
            relay(t)

        c = t - LAG

        @pl.when(c > 0)
        def _():
            forward(c - 1, 0)

        @pl.when((c >= 0) & (c < CHUNKS))
        def _():
            relay_out(c, 0).wait_recv()
            if spill:
                far_tail(c).start()

        @pl.when(c > 0)
        def _():
            attend(c - 1)

        @pl.when((c >= 0) & (c < CHUNKS))
        def _():
            @pl.when(c == 0)
            def _():
                own_copy.wait()
                q_copy.wait()

            if spill:
                far_tail(c).wait_recv()

            for part in range(2):
                settle(landing.at[pl.ds(0, n_half - 1), :, part_cols(c, part)], fetch_recv.at[c, part])
                blend(c, part)
                for b in range(1, n_chips):
                    @pl.when(chip < b)
                    def _():
                        gather(c, b, part).start()

                @pl.when(core == 0)
                def _():
                    pair(c, part).start()


        return carry

    lax.fori_loop(0, CHUNKS + LAG + 1, step, 0)

    settle(landing.at[pl.ds(0, n_half - 1)], fetch_send)

    @pl.when(is_relay)
    def _():
        settle(relay_in.at[:, pl.ds(0, ny - 1)], relay_send)
        settle(merged, merged_send)
        if spill:
            settle(tail_out, tail_send)

    @pl.when(jnp.logical_not(is_relay))
    def _():
        settle(relay_in.at[:, pl.ds(0, ny)], relay_send)

    if spill:
        settle(tail_in.at[0], spill_send)

    for b in range(1, n_chips):
        @pl.when(chip < b)
        def _():
            settle(kv_all.at[0], gather_send.at[b])

    for a in range(n_chips - 1):
        @pl.when(a < chip)
        def _():
            settle(kv_all.at[0], forward_send.at[a])

    @pl.when(core == 0)
    def _():
        settle(kv_all.at[0], pair_send)


def on_device(n_store, n_seq, store_kv, span_len, span_shard, q_sel, fresh_kv, sel_pos):
    slot_rows = store_kv.shape[1]
    tok = 256
    sel = sel_pos.shape[1]
    half = np.arange(D_HEAD // 2, dtype=np.float64) * 2.0 / D_HEAD
    inverse = np.power(ROPE_BASE, -np.concatenate([half, half]))[None].astype(np.float32)
    hbm = pl.BlockSpec(memory_space=pl.ANY)
    dma = pltpu.SemaphoreType.DMA
    bf16 = jnp.bfloat16
    n_chips = n_seq // 2
    n_half = n_store // 2
    keep_rows = frame_rows(n_store, slot_rows, tok)
    spill = tok - keep_rows
    return pl.pallas_call(
        functools.partial(kernel, n_store, n_seq),
        out_shape=(
            pltpu.VMEM((1, tok, 2 * KV_WIDTH), bf16),
            pltpu.VMEM((1, sel, HEADS * D_HEAD), bf16),
        ),
        in_specs=[hbm] * 7,
        out_specs=(pl.BlockSpec(memory_space=pltpu.VMEM),) * 2,
        scratch_shapes=[
            pltpu.VMEM(span_len.shape, jnp.int32),
            pltpu.VMEM(span_shard.shape, jnp.int32),
            pltpu.VMEM(inverse.shape, F32),
            pltpu.VMEM(fresh_kv.shape, bf16),
            pltpu.VMEM(sel_pos.shape, jnp.int32),
            pltpu.VMEM((n_half, slot_rows, 2 * KV_WIDTH), bf16),
            pltpu.VMEM((2, n_half, slot_rows, 2 * KV_WIDTH), bf16),
            pltpu.VMEM((2, CHUNKS, keep_rows, 2 * CW), bf16),
            pltpu.VMEM((CHUNKS, tok, 2 * CW), bf16),
            pltpu.VMEM((n_seq, CHUNKS, 2, tok, CW), bf16),
            pltpu.VMEM((sel, HEADS * D_HEAD), bf16),
            pltpu.VMEM((n_seq, GROUPS * sel, tok), F32),
            pltpu.VMEM((tok, n_half * slot_rows), bf16),
            pltpu.VMEM((tok, tok), bf16),
            pltpu.VMEM((2, tok, n_half * slot_rows), bf16),
            pltpu.VMEM((tok, sel), bf16),
            pltpu.VMEM((2, CHUNKS, spill, 2 * CW), bf16),
            pltpu.VMEM((2, CHUNKS, spill, 2 * CW), bf16),
            pltpu.VMEM((tok, D_HEAD), F32),
            pltpu.VMEM((tok, D_HEAD), F32),
            pltpu.VMEM((tok, D_HEAD), F32),
            pltpu.VMEM((sel, D_HEAD), F32),
            dma(()),
            dma((CHUNKS, 2)),
            dma(()),
            dma((CHUNKS, 2)),
            dma(()),
            dma((CHUNKS,)),
            dma(()),
            dma((CHUNKS,)),
            dma(()),
            dma((CHUNKS,)),
            dma((3,)),
            dma(()),
            dma((n_chips,)),
            dma((CHUNKS, n_chips - 1, 2)),
            dma((CHUNKS, n_chips - 1, 2)),
            dma((CHUNKS, 2)),
            dma((n_chips,)),
            dma(()),
            dma((5,)),
        ],
        compiler_params=pltpu.CompilerParams(
            collective_id=0, has_side_effects=True, vmem_limit_bytes=60 * 1024 * 1024
        ),
    )(store_kv, span_len, span_shard, jnp.asarray(inverse), q_sel, fresh_kv, sel_pos)


def solution(mesh):
    n_store, n_seq = mesh.shape["store"], mesh.shape["seq"]
    return jax.shard_map(
        functools.partial(on_device, n_store, n_seq),
        mesh=mesh,
        in_specs=(
            P("store", "seq", None),
            P(),
            P(),
            P("store", "seq", None),
            P("store", "seq", None),
            P("store", "seq"),
        ),
        out_specs=(P("store", "seq", None), P("store", "seq", None)),
        check_vma=False,
    )
```

time: 72.5 us -> 67.5 us (0.931)
  Pallas kernels: 68.3 us -> 64.8 us
  local copies, waits for them, and re-layouts: 3.37 us -> 1.94 us
    pallas_call x1, Pallas kernels: 68.3 us -> 64.8 us  [on_device(): pl.pallas_call(functools.partial(kernel, n_store, n_seq), out_shape=(pltp...]
    unnamed x4 -> x2, local copies, waits for them, and re-layouts: 3.37 us -> 1.94 us
where the time goes in v2:
time: 67.5 us; the launch traced here: 67.4 us
  Pallas kernels  64.8 us (96%)
  local copies, waits for them, and re-layouts  1.94 us (3%)
    pallas_call x1, Pallas kernels, on_device(): pl.pallas_call(functools.partial(kernel, n_store, n_seq), out_shape=(pltp...  64.8 us
    unnamed x2, local copies, waits for them, and re-layouts  1.94 us

profile of v2, /device:TPU:11, one launch (start us, length us, event | category | flops | bytes accessed | tf_op | source)
XLA Modules:
  0.0 67.4 jit_solution(13649882112255600045)
XLA Ops:
  0.6 64.8 %shard_map.86 = (bf16[1,256,2048]{2,1,0:T(8,128)(2,1)S(1)}, bf16[1,64,8192]{2,1,0:T(8,128)(2,1)S(1)}) custom-call(bf16[8,80,2048]{2,1,0:T(8,128)(2,1)} %store_ref.1, s32[8,16]{1,0:T(8,128)} %len_hbm.1, s32[8,8]{1,0:T(8,128)} %shard_hbm.1, f32[1,128]{1,0:T(1,128)} %constant.2.clone.inv_hbm, bf16[1,64,8192]{2,1,0:T(8,128)(2,1)} %q_ref.1, ...), custom_call_target="tpu_custom_call" | custom-call | tf_op jit(solution)/shard_map/pallas_call | solution.py:496
  65.4 1.0 %copy.11 = bf16[1,256,2048]{2,1,0:T(8,128)(2,1)} copy(bf16[1,256,2048]{2,1,0:T(8,128)(2,1)S(1)} %get-tuple-element.2) | data formatting | bytes 2097152
  66.4 1.0 %copy.12 = bf16[1,64,8192]{2,1,0:T(8,128)(2,1)} copy(bf16[1,64,8192]{2,1,0:T(8,128)(2,1)S(1)} %get-tuple-element.3) | data formatting | bytes 2097152

commit v3 on v2

--- a/solution.py
+++ b/solution.py
@@ -16,8 +16,9 @@
 KV_WIDTH = KV_HEADS * D_HEAD
 ROPE_BASE = 500000.0
 CHUNKS = KV_HEADS
-LAG = 2
-LEAD = 2
+LEAD = 3
+BURST = 5
+SPAN = 4
 SHORTEST, LONGEST = 37, 80
 CW = D_HEAD
 F32 = jnp.float32
@@ -183,20 +184,21 @@
                 for d in range(1, ny):
                     act(to_relay(c, local, (lane + d) % ny, j, part))
 
-    def issue(t, carry):
-        @pl.when(t < CHUNKS)
-        def _():
-            each_to_relay(t, lambda copy: copy.start())
-
-        @pl.when(t >= LEAD)
-        def _():
-            for d in range(1, n_half):
-                for part in range(2):
-                    fetch(t - LEAD, local, (local + d) % n_half, part).start()
-
+    def relayed(c):
+        return jnp.where(c < 0, 0, jnp.where(c < BURST, jnp.minimum(c + LEAD, CHUNKS), CHUNKS))
+
+    def issue(c, carry):
+        def feed(r, carry):
+            each_to_relay(r, lambda copy: copy.start())
+            return carry
+
+        lax.fori_loop(relayed(c - 1), relayed(c), feed, 0)
+        for d in range(1, n_half):
+            for part in range(2):
+                fetch(c, local, (local + d) % n_half, part).start()
         return carry
 
-    lax.fori_loop(0, CHUNKS + LEAD, issue, 0)
+    lax.fori_loop(0, CHUNKS, issue, 0)
     own_copy.start()
 
     @pl.when(is_relay)
@@ -336,43 +338,62 @@
 
     def attend(c):
         base = c * GROUPS * D_HEAD
-        wide = qv[:, pl.ds(pl.multiple_of(base, GROUPS * D_HEAD), GROUPS * D_HEAD)]
-        q = jnp.concatenate([wide[:, g * D_HEAD:(g + 1) * D_HEAD] for g in range(GROUPS)], axis=0)
-
-        def scores_of(s):
+        rows = GROUPS * sel
+
+        def queries():
+            wide = qv[:, pl.ds(pl.multiple_of(base, GROUPS * D_HEAD), GROUPS * D_HEAD)]
+            return jnp.concatenate([wide[:, g * D_HEAD:(g + 1) * D_HEAD] for g in range(GROUPS)], axis=0)
+
+        def scores_of(q, s):
             return lax.dot_general(q, kv_all[s, c, 0], contract, preferred_element_type=F32)
 
-        own = scores_of(stripe)
-        keep = iota((sel, tok), 1).astype(F32) + first <= limit[:, 0:1]
-        keep = jnp.concatenate([jnp.where(keep, 0.0, -1e30)] * GROUPS, axis=0)
-        own = jnp.where(keep < 0.0, -1e30, own)
-        scores[stripe] = own
-        await_sibling(c, 0)
-
-        def score(s, top):
-            x = scores_of(s)
-            scores[s] = x
-            return jnp.maximum(top, peak_of(x))
-
-        top = lax.fori_loop(0, stripe, score, peak_of(own))
-        top = jnp.max(top, axis=1, keepdims=True) * scale
-        forward(c, 1)
-        ones = jnp.ones((tok, D_HEAD), jnp.bfloat16)
-
-        def weighted(s):
-            weights = jnp.exp2(scores[s] * scale - top).astype(jnp.bfloat16)
-            return jnp.dot(
-                weights, jnp.concatenate([kv_all[s, c, 1], ones], axis=1), preferred_element_type=F32
-            )
-
-        acc = weighted(stripe)
-        await_sibling(c, 1)
-        acc = lax.fori_loop(0, stripe, lambda s, acc: acc + weighted(s), acc)
-        normed = acc[:, :D_HEAD] * (1.0 / acc[:, D_HEAD:])
-        live = limit[...] >= 0.0
-        for g in range(GROUPS):
-            part = jnp.where(live, normed[g * sel:(g + 1) * sel], 0.0)
-            attn_out[0, :, pl.ds(pl.multiple_of(base + g * D_HEAD, D_HEAD), D_HEAD)] = part.astype(jnp.bfloat16)
+        def weights_of(x, top):
+            return jnp.exp2(x * scale - top).astype(jnp.bfloat16)
+
+        def with_ones(v):
+            return jnp.concatenate([v, jnp.ones_like(v)], axis=1)
+
+        def group(late):
+            q = queries()
+            begin = stripe - late
+            own = scores_of(q, stripe)
+            keep = iota((sel, tok), 1).astype(F32) + first <= limit[:, 0:1]
+            keep = jnp.concatenate([jnp.where(keep, 0.0, -1e30)] * GROUPS, axis=0)
+            own = jnp.where(keep < 0.0, -1e30, own)
+            await_sibling(c, 0)
+            found = [scores_of(q, begin + i) for i in range(late)] + [own]
+            top = functools.reduce(jnp.maximum, [peak_of(x) for x in found])
+            if n_seq > SPAN:
+                def score(s, top):
+                    x = scores_of(q, s)
+                    scores[s] = x
+                    return jnp.maximum(top, peak_of(x))
+
+                top = lax.fori_loop(0, begin, score, top)
+            top = jnp.max(top, axis=1, keepdims=True) * scale
+            weights = jnp.concatenate([weights_of(x, top) for x in found], axis=1)
+
+            @pl.when(c == CHUNKS - 1)
+            def _():
+                forward(c, 1)
+
+            await_sibling(c, 1)
+            values = kv_all[pl.ds(begin, late + 1), c, 1].reshape((late + 1) * tok, D_HEAD)
+            acc = jnp.dot(weights, with_ones(values), preferred_element_type=F32)
+            if n_seq > SPAN:
+                acc = lax.fori_loop(0, begin, lambda s, acc: acc + jnp.dot(
+                    weights_of(scores[s], top), with_ones(kv_all[s, c, 1]), preferred_element_type=F32
+                ), acc)
+            normed = acc[:, :D_HEAD] * (1.0 / acc[:, D_HEAD:])
+            live = limit[...] >= 0.0
+            for g in range(GROUPS):
+                part = jnp.where(live, normed[g * sel:(g + 1) * sel], 0.0)
+                attn_out[0, :, pl.ds(pl.multiple_of(base + g * D_HEAD, D_HEAD), D_HEAD)] = part.astype(jnp.bfloat16)
+
+        for late in range(min(n_seq, SPAN)):
+            @pl.when(stripe % SPAN == late)
+            def _():
+                group(late)
 
     def relay(c):
         for part in range(2):
@@ -394,6 +415,7 @@
             if spill:
                 relay_tail(c, j).start()
 
+    def send_on(c):
         if spill:
             settle(tail_in.at[:, c], tail_recv.at[c])
         for j in range(2):
@@ -401,28 +423,43 @@
                 merged[j, c, keep_rows - spill:] = merged[j, c, keep_rows - spill:] + tail_in[j, c]
             relay_out(c, j).start()
 
-    def step(t, carry):
-        @pl.when((t < CHUNKS) & is_relay)
-        def _():
-            relay(t)
-
-        c = t - LAG
+    def step(c, carry):
+        def merge(r, carry):
+            relay(r)
+            send_on(r)
+            return carry
+
+        newest = relayed(c) - 1
+        merging = is_relay & (newest >= relayed(c - 1))
+
+        @pl.when(merging)
+        def _():
+            lax.fori_loop(relayed(c - 1), newest, merge, 0)
+            relay(newest)
 
         @pl.when(c > 0)
         def _():
             forward(c - 1, 0)
 
-        @pl.when((c >= 0) & (c < CHUNKS))
+        @pl.when(merging)
+        def _():
+            send_on(newest)
+
+        @pl.when(c < CHUNKS)
         def _():
             relay_out(c, 0).wait_recv()
             if spill:
                 far_tail(c).start()
 
+        @pl.when((c > 0) & (c < CHUNKS))
+        def _():
+            forward(c - 1, 1)
+
         @pl.when(c > 0)
         def _():
             attend(c - 1)
 
-        @pl.when((c >= 0) & (c < CHUNKS))
+        @pl.when(c < CHUNKS)
         def _():
             @pl.when(c == 0)
             def _():
@@ -444,10 +481,9 @@
                 def _():
                     pair(c, part).start()
 
-
         return carry
 
-    lax.fori_loop(0, CHUNKS + LAG + 1, step, 0)
+    lax.fori_loop(0, CHUNKS + 1, step, 0)
 
     settle(landing.at[pl.ds(0, n_half - 1)], fetch_send)
 
@@ -513,7 +549,7 @@
             pltpu.VMEM((CHUNKS, tok, 2 * CW), bf16),
             pltpu.VMEM((n_seq, CHUNKS, 2, tok, CW), bf16),
             pltpu.VMEM((sel, HEADS * D_HEAD), bf16),
-            pltpu.VMEM((n_seq, GROUPS * sel, tok), F32),
+            pltpu.VMEM((max(n_seq - SPAN, 1), GROUPS * sel, tok), F32),
             pltpu.VMEM((tok, n_half * slot_rows), bf16),
             pltpu.VMEM((tok, tok), bf16),
             pltpu.VMEM((2, tok, n_half * slot_rows), bf16),

time: 67.5 us -> 63.9 us (0.947)
  Pallas kernels: 64.8 us -> 61.1 us
    pallas_call x1, Pallas kernels: 64.8 us -> 61.1 us  [on_device(): pl.pallas_call(functools.partial(kernel, n_store, n_seq), out_shape=(pltp...]
where the time goes in v3:
time: 63.9 us; the launch traced here: 63.7 us
  Pallas kernels  61.1 us (96%)
  local copies, waits for them, and re-layouts  1.94 us (3%)
  between operations  0.64 us (1%)
    pallas_call x1, Pallas kernels, on_device(): pl.pallas_call(functools.partial(kernel, n_store, n_seq), out_shape=(pltp...  61.1 us
    unnamed x2, local copies, waits for them, and re-layouts  1.94 us

profile of v3, /device:TPU:11, one launch (start us, length us, event | category | flops | bytes accessed | tf_op | source)
XLA Modules:
  0.0 63.7 jit_solution(3481032872978293159)
XLA Ops:
  0.6 61.1 %shard_map.86 = (bf16[1,256,2048]{2,1,0:T(8,128)(2,1)S(1)}, bf16[1,64,8192]{2,1,0:T(8,128)(2,1)S(1)}) custom-call(bf16[8,80,2048]{2,1,0:T(8,128)(2,1)} %store_ref.1, s32[8,16]{1,0:T(8,128)} %len_hbm.1, s32[8,8]{1,0:T(8,128)} %shard_hbm.1, f32[1,128]{1,0:T(1,128)} %constant.2.clone.inv_hbm, bf16[1,64,8192]{2,1,0:T(8,128)(2,1)} %q_ref.1, ...), custom_call_target="tpu_custom_call" | custom-call | tf_op jit(solution)/shard_map/pallas_call | solution.py:532
  61.8 1.0 %copy.11 = bf16[1,256,2048]{2,1,0:T(8,128)(2,1)} copy(bf16[1,256,2048]{2,1,0:T(8,128)(2,1)S(1)} %get-tuple-element.2) | data formatting | bytes 2097152
  62.7 1.0 %copy.12 = bf16[1,64,8192]{2,1,0:T(8,128)(2,1)} copy(bf16[1,64,8192]{2,1,0:T(8,128)(2,1)S(1)} %get-tuple-element.3) | data formatting | bytes 2097152

commit v4 on v3

--- a/solution.py
+++ b/solution.py
@@ -17,8 +17,9 @@
 ROPE_BASE = 500000.0
 CHUNKS = KV_HEADS
 LEAD = 3
-BURST = 5
+BURST = 8
 SPAN = 4
+PIECES = 4
 SHORTEST, LONGEST = 37, 80
 CW = D_HEAD
 F32 = jnp.float32
@@ -405,13 +406,13 @@
                 own_relay(j).wait()
 
         for j in range(2):
-            for part in range(2):
-                slots = relay_in[j, :, :, part_cols(c, part)].reshape(n_half * slot_rows, CW)
-                rows = jnp.dot(relay_pick[j], slots, preferred_element_type=F32)
-                cols = slice(part * CW, (part + 1) * CW)
-                merged[j, c, :, cols] = rows[:keep_rows].astype(jnp.bfloat16)
-                if spill:
-                    tail_out[j, c, :, cols] = rows[keep_rows:].astype(jnp.bfloat16)
+            slots = jnp.concatenate([
+                relay_in[j, :, :, part_cols(c, part)].reshape(n_half * slot_rows, CW) for part in range(2)
+            ], axis=1)
+            rows = jnp.dot(relay_pick[j], slots, preferred_element_type=F32)
+            merged[j, c] = rows[:keep_rows].astype(jnp.bfloat16)
+            if spill:
+                tail_out[j, c] = rows[keep_rows:].astype(jnp.bfloat16)
             if spill:
                 relay_tail(c, j).start()
 
@@ -455,10 +456,6 @@
         def _():
             forward(c - 1, 1)
 
-        @pl.when(c > 0)
-        def _():
-            attend(c - 1)
-
         @pl.when(c < CHUNKS)
         def _():
             @pl.when(c == 0)
@@ -481,6 +478,10 @@
                 def _():
                     pair(c, part).start()
 
+        @pl.when(c > 0)
+        def _():
+            attend(c - 1)
+
         return carry
 
     lax.fori_loop(0, CHUNKS + 1, step, 0)
@@ -514,6 +515,19 @@
     @pl.when(core == 0)
     def _():
         settle(kv_all.at[0], pair_send)
+
+
+def write_out(kv_ref, attn_ref, kv_out, attn_out, sems):
+    copies = []
+    for i, (src, dst) in enumerate(((kv_ref, kv_out), (attn_ref, attn_out))):
+        rows = src.shape[1] // PIECES
+        for p in range(PIECES):
+            at = pl.ds(p * rows, rows)
+            copies.append(pltpu.make_async_copy(src.at[0, at], dst.at[0, at], sems.at[i, p]))
+    for copy in copies:
+        copy.start()
+    for copy in copies:
+        copy.wait()
 
 
 def on_device(n_store, n_seq, store_kv, span_len, span_shard, q_sel, fresh_kv, sel_pos):
@@ -529,7 +543,7 @@
     n_half = n_store // 2
     keep_rows = frame_rows(n_store, slot_rows, tok)
     spill = tok - keep_rows
-    return pl.pallas_call(
+    kv, attn = pl.pallas_call(
         functools.partial(kernel, n_store, n_seq),
         out_shape=(
             pltpu.VMEM((1, tok, 2 * KV_WIDTH), bf16),
@@ -584,6 +598,14 @@
             collective_id=0, has_side_effects=True, vmem_limit_bytes=60 * 1024 * 1024
         ),
     )(store_kv, span_len, span_shard, jnp.asarray(inverse), q_sel, fresh_kv, sel_pos)
+    return pl.pallas_call(
+        write_out,
+        out_shape=(jax.ShapeDtypeStruct(kv.shape, bf16), jax.ShapeDtypeStruct(attn.shape, bf16)),
+        in_specs=[pl.BlockSpec(memory_space=pltpu.VMEM)] * 2,
+        out_specs=(hbm, hbm),
+        scratch_shapes=[dma((2, PIECES))],
+        compiler_params=pltpu.CompilerParams(has_side_effects=True),
+    )(*(pltpu.with_memory_space_constraint(x, pltpu.VMEM) for x in (kv, attn)))
 
 
 def solution(mesh):

time: 63.9 us -> 62.3 us (0.975)
  local copies, waits for them, and re-layouts: 1.94 us -> 0 us
    unnamed x2 -> x0, local copies, waits for them, and re-layouts: 1.94 us -> none
    pallas_call x0 -> x1, Pallas kernels: none -> 1.38 us  [on_device(): pl.pallas_call(write_out, out_shape=(jax.ShapeDtypeStruct(kv.shape, bf16)...]
    pallas_call x1, Pallas kernels: 61.1 us -> 60.1 us  [on_device(): pl.pallas_call(functools.partial(kernel, n_store, n_seq), out_shape=(pltp...]
where the time goes in v4:
time: 62.3 us; the launch traced here: 62.1 us
  Pallas kernels  61.5 us (99%)
  between operations  0.64 us (1%)
    pallas_call x1, Pallas kernels, on_device(): pl.pallas_call(functools.partial(kernel, n_store, n_seq), out_shape=(pltp...  60.1 us
    pallas_call x1, Pallas kernels, on_device(): pl.pallas_call(write_out, out_shape=(jax.ShapeDtypeStruct(kv.shape, bf16)...  1.38 us

profile of v4, /device:TPU:11, one launch (start us, length us, event | category | flops | bytes accessed | tf_op | source)
XLA Modules:
  0.0 62.1 jit_solution(3796978725375659864)
XLA Ops:
  0.6 60.1 %shard_map.86 = (bf16[1,256,2048]{2,1,0:T(8,128)(2,1)S(1)}, bf16[1,64,8192]{2,1,0:T(8,128)(2,1)S(1)}) custom-call(bf16[8,80,2048]{2,1,0:T(8,128)(2,1)} %store_ref.1, s32[8,16]{1,0:T(8,128)} %len_hbm.1, s32[8,8]{1,0:T(8,128)} %shard_hbm.1, f32[1,128]{1,0:T(1,128)} %constant.2.clone.inv_hbm, bf16[1,64,8192]{2,1,0:T(8,128)(2,1)} %q_ref.1, ...), custom_call_target="tpu_custom_call" | custom-call | tf_op jit(solution)/shard_map/pallas_call | solution.py:546
  60.8 1.4 %shard_map.87 = (bf16[1,256,2048]{2,1,0:T(8,128)(2,1)}, bf16[1,64,8192]{2,1,0:T(8,128)(2,1)}) custom-call(bf16[1,256,2048]{2,1,0:T(8,128)(2,1)S(1)} %get-tuple-element.4.kv_ref, bf16[1,64,8192]{2,1,0:T(8,128)(2,1)S(1)} %get-tuple-element.5.attn_ref), custom_call_target="tpu_custom_call" | custom-call | tf_op jit(solution)/shard_map/pallas_call | solution.py:601
